TPU v7x, 256 devices: a whole 4x4x8 slice. The times are simulated.
256 devices in a mesh: seq: 8 (over z), chan: 32 (over y, x, core).
Axes of the slice: x: 4, y: 4, z: 8, core: 2. Of those that a mesh axis runs over, the one named last changes fastest.
Arguments:
- tokens: bfloat16 [8192, 4096], P('seq', 'chan'), may hold values from -8 to 8
- norm_gain: float32 [4096], replicated, may hold values from 0.5 to 1.5
- gate_proj: bfloat16 [4096, 8192], P(None, 'chan'), may hold values from -0.09375 to 0.09375
- inner_proj: bfloat16 [4096, 8192], P(None, 'chan'), may hold values from -0.09375 to 0.09375
- state_proj: bfloat16 [4096, 384], P('chan'), may hold values from -0.11816406 to 0.11816406
- conv_inner: float32 [4, 8192], P(None, 'chan'), may hold values from -3 to 3
- conv_state: float32 [4, 256], replicated, may hold values from -3 to 3
- log_rate: float32 [128], P('chan'), may hold values from -1 to 0
- rate_bias: float32 [128], P('chan'), may hold values from -16 to -2
- skip_gain: float32 [128], P('chan'), may hold values from 0.2 to 4
- gate_gain: float32 [8192], P('chan'), may hold values from 0.5 to 1.5
- out_proj: bfloat16 [8192, 4096], P('chan'), may hold values from -0.125 to 0.125
Outputs:
- layer_out: bfloat16 [8192, 4096], P('seq', 'chan')
All inputs are finite; a program needn't handle non-finite values.
Results may differ from a plain program's by a relative error of at most 0.012.
Values may be sent and summed in bfloat16 or wider, within the bound.
A program may use at most 128 MiB of HBM per device.

v0:
```python
import jax
import jax.numpy as jnp
from jax import lax
from jax.sharding import PartitionSpec as P

P_SIZE = 64
N = 128
K = 4
Q = 256
DI = 8192


def from_behind(value, axis, steps):
    count = lax.axis_size(axis)
    leading, last = (max(0, -steps), min(count, count - steps))
    return lax.ppermute(value, axis, [(source, source + steps) for source in range(leading, last)])


def prefix(value, axis, join, neutral):
    count, mine = (lax.axis_size(axis), lax.axis_index(axis))
    pieces = jax.tree.map(lambda part: lax.all_gather(part, axis), value)
    total = jax.tree.map(
        lambda part, zero: jnp.full_like(part, 0) + jnp.asarray(zero, part.dtype), value, neutral
    )

    def turn(position, total):
        longer = join(total, jax.tree.map(lambda part: part[position], pieces))
        return jax.tree.map(lambda new, old: jnp.where(position < mine, new, old), longer, total)

    return lax.fori_loop(0, count - 1, turn, total)


def from_everyone(x, axis):
    size = lax.axis_size(axis)
    return lax.all_to_all(jnp.broadcast_to(x[None], (size, *x.shape)), axis, 0, 0, tiled=True)


def over_copies(x, axis):
    everything = from_everyone(x, axis)
    return jnp.sum(everything, axis=0)


def causal_mix(rim_part, fresh_rows, weights):
    length = fresh_rows.shape[0]
    padded = jnp.concatenate([rim_part.astype(jnp.float32), fresh_rows.astype(jnp.float32)], axis=0)
    summed = jnp.zeros(fresh_rows.shape, jnp.float32)
    for offset in range(weights.shape[0]):
        summed = summed + weights[offset] * padded[offset : offset + length]
    return jax.nn.silu(summed)


def combine_pair(earlier_part, later_part):
    return (
        earlier_part[0] * later_part[0],
        later_part[0][:, None, None] * earlier_part[1] + later_part[1],
    )


def local(
    tokens,
    norm_gain,
    gate_proj,
    inner_proj,
    state_proj,
    conv_inner,
    conv_state,
    log_rate,
    rate_bias,
    skip_gain,
    gate_gain,
    out_proj,
):
    gathered = lax.all_gather(tokens, "chan", axis=1, tiled=True)
    widened = gathered.astype(jnp.float32)
    inverse = lax.rsqrt(jnp.mean(widened * widened, axis=1, keepdims=True) + 1e-05)
    normed = (widened * inverse * norm_gain).astype(jnp.bfloat16)
    gate_raw = jnp.dot(normed, gate_proj, preferred_element_type=jnp.float32).astype(jnp.bfloat16)
    inner_raw = jnp.dot(normed, inner_proj, preferred_element_type=jnp.float32).astype(jnp.bfloat16)
    heads = log_rate.shape[0]
    start_head = lax.axis_index("chan") * heads
    projected = jnp.dot(
        normed,
        lax.all_gather(state_proj, "chan", axis=0, tiled=True),
        preferred_element_type=jnp.float32,
    )
    state_raw = projected[:, : 2 * N]
    raw_rate = lax.dynamic_slice_in_dim(projected, 2 * N + start_head, heads, 1)
    rim_rows = from_behind(
        (inner_raw[-(K - 1) :].astype(jnp.float32), state_raw[-(K - 1) :]), "seq", 1
    )
    inner_conv = causal_mix(rim_rows[0].astype(jnp.bfloat16), inner_raw, conv_inner)
    state_conv = causal_mix(rim_rows[1], state_raw, conv_state)
    token_rows = tokens.shape[0]
    blocks = token_rows // Q
    step_size = jax.nn.softplus(raw_rate + rate_bias)
    decay_log = -jnp.exp(log_rate) * step_size
    values = inner_conv.reshape(blocks, Q, heads, P_SIZE)
    in_map = state_conv[:, :N].reshape(blocks, Q, N)
    out_map = state_conv[:, N:].reshape(blocks, Q, N)
    step_rows = step_size.reshape(blocks, Q, heads).transpose(0, 2, 1)
    log_rows = decay_log.reshape(blocks, Q, heads).transpose(0, 2, 1)
    lower_mask = (jnp.arange(Q)[:, None] >= jnp.arange(Q)[None, :]).astype(jnp.float32)
    within = jnp.einsum("chs,ts->cht", log_rows, lower_mask)
    log_gaps = within[..., :, None] - within[..., None, :]
    fading = jnp.exp(jnp.where(lower_mask > 0, log_gaps, -jnp.inf))
    scores = jnp.einsum("ctn,csn->cts", out_map, in_map)
    mixing = scores[:, None] * fading * step_rows[:, :, None, :]
    local_out = jnp.einsum("chts,cshp->cthp", mixing, values)
    tail_weight = jnp.exp(within[..., -1:] - within) * step_rows
    scaled = values * tail_weight.transpose(0, 2, 1)[..., None]
    block_end = jnp.einsum("csn,cshp->chnp", in_map, scaled)
    block_log = within[..., -1]
    through = jnp.cumsum(block_log, axis=0)
    before = through - block_log
    earlier = jnp.arange(blocks)[:, None] > jnp.arange(blocks)[None, :]
    passage = jnp.exp(
        jnp.where(earlier[:, :, None], before[:, None, :] - through[None, :, :], -jnp.inf)
    )
    entering = jnp.einsum("cdh,dhnp->chnp", passage, block_end)
    device_end = jnp.einsum("ch,chnp->hnp", jnp.exp(through[-1:] - through), block_end)
    device_fade = jnp.exp(through[-1])
    identity = (jnp.ones_like(device_fade), jnp.zeros_like(device_end))
    carried = prefix((device_fade, device_end), "seq", combine_pair, identity)[1]
    entering = entering + jnp.exp(before)[:, :, None, None] * carried[None]
    carried_out = jnp.einsum("ctn,chnp->cthp", out_map, entering)
    carried_out = carried_out * jnp.exp(within).transpose(0, 2, 1)[..., None]
    skip_wide = jnp.repeat(skip_gain, P_SIZE)
    ssd_out = (local_out + carried_out).reshape(token_rows, heads * P_SIZE) + skip_wide * inner_conv
    gated_out = ssd_out * jax.nn.silu(gate_raw.astype(jnp.float32))
    energy = over_copies(jnp.sum(gated_out * gated_out, axis=1), "chan")
    norm_scale = lax.rsqrt(energy / DI + 1e-05)
    shaped = (gated_out * norm_scale[:, None] * gate_gain).astype(jnp.bfloat16)
    column_rows = lax.all_to_all(out_proj, "chan", split_axis=1, concat_axis=0, tiled=True)
    summed = jnp.dot(
        lax.all_gather(shaped, "chan", axis=1, tiled=True),
        column_rows,
        preferred_element_type=jnp.float32,
    )
    return (tokens.astype(jnp.float32) + summed).astype(jnp.bfloat16)


def solution(mesh):
    return jax.shard_map(
        local,
        mesh=mesh,
        in_specs=(
            P("seq", "chan"),
            P(),
            P(None, "chan"),
            P(None, "chan"),
            P("chan", None),
            P(None, "chan"),
            P(),
            P("chan"),
            P("chan"),
            P("chan"),
            P("chan"),
            P("chan", None),
        ),
        out_specs=P("seq", "chan"),
        check_vma=False,
    )
```

profile of v0, /device:TPU:1, one launch (start us, length us, event | category | flops | bytes accessed | tf_op | source)
XLA Modules:
  0.0 364.0 jit_solution(8693260345117643009)
XLA Ops:
  10.4 67.4 %all-gather.7.cloned.1.call-done = bf16[1024,4096]{1,0:T(8,128)(2,1)} async-done(((bf16[1024,128]{1,0:T(8,128)(2,1)}), bf16[1024,4096]{1,0:T(8,128)(2,1)}) %all-gather.7.cloned.1.call-update) | async-done | bytes 8388624 | tf_op jit(solution)/shard_map/all_gather | solution.py:73
  77.8 5.1 %fusion.1 = f32[1024]{0:T(1024)S(1)} fusion(bf16[1024,4096]{1,0:T(8,128)(2,1)} %all-gather.7.cloned.1.call-done), kind=kLoop, calls=%fused_computation.6 | loop fusion | flops 12581888 | bytes 8392704 | tf_op jit(solution)/shard_map/reduce_sum | solution.py:75
  82.9 47.1 %all-gather.9.cloned.1.call-done = bf16[4096,384]{1,0:T(8,128)(2,1)} async-done(((bf16[128,384]{1,0:T(8,128)(2,1)}), bf16[4096,384]{1,0:T(8,128)(2,1)}) %all-gather.9.cloned.1.call-update) | async-done | bytes 3145744 | tf_op jit(solution)/shard_map/all_gather | solution.py:83
  130.0 8.1 %fusion.63 = f32[1024,384]{1,0:T(8,128)S(1)} fusion(bf16[4096,384]{1,0:T(8,128)(2,1)} %all-gather.9.cloned.1.call-done, bf16[1024,4096]{1,0:T(8,128)(2,1)} %all-gather.7.cloned.1.call-done, f32[4096]{0:T(1024)S(1)} %copy-done.10, f32[1024]{0:T(1024)S(1)} %add_rsqrt_fusion.1), kind=kOutput, calls=%fused_computation.97 | convolution fusion | flops 3238002688 | bytes 13127680 | tf_op jit(solution)/shard_map/dot_general | solution.py:81
  138.1 3.2 collective-permute-start.1
  142.3 5.9 %fusion.70 = (f32[1024,256]{1,0:T(8,128)S(1)}, bf16[1024,256]{1,0:T(8,128)(2,1)S(1)}) fusion(bf16[4096,256]{1,0:T(8,128)(2,1)S(1)} %copy-done, bf16[1024,4096]{1,0:T(8,128)(2,1)} %all-gather.7.cloned.1.call-done, f32[4096]{0:T(1024)S(1)} %copy-done.10, f32[1024]{0:T(1024)S(1)} %add_rsqrt_fusion.1), kind=kOutput, calls=%fused_computation.102 | convolution fusion | flops 2164785152 | bytes 12079104 | tf_op jit(solution)/shard_map/dot_general | solution.py:78
  148.2 3.2 collective-permute-start
  151.5 1.1 slice.93
  153.2 1.3 copy.120
  154.5 2.8 reshape.81
  157.3 1.4 broadcast_multiply_fusion
  158.7 3.1 divide_multiply_fusion
  162.6 0.9 fusion.47
  164.2 12.4 %all-gather.1 = f32[8,1,4]{2,1,0:T(1,128)S(1)} all-gather(f32[1,1,4]{2,1,0:T(1,128)S(1)} %get-tuple-element.179), channel_id=1, replica_groups=mesh['seq'=8,'chan'=32] {'seq'}, dimensions={0}, use_global_device_ids=true | all-gather | bytes 144 | tf_op jit(solution)/shard_map/all_gather | solution.py:21
  176.6 2.2 fusion.71
  178.8 19.2 %all-gather.13.cloned.1.call-done = f32[32,128,64]{1,2,0:T(8,128)} async-done(((f32[4,128,64]{1,2,0:T(8,128)}), f32[32,128,64]{1,2,0:T(8,128)}) %all-gather.13.cloned.1.call-update) | async-done | bytes 1048592 | tf_op jit(solution)/shard_map/all_gather | solution.py:21
  198.0 8.4 %while.14 = (s32[]{:T(128)}, f32[4,128,64]{2,1,0:T(8,128)S(1)}, s32[]{:T(128)}, f32[8,4]{1,0:T(8,128)S(1)}, f32[8,4,128,64]{2,3,1,0:T(8,128)}, /*index=5*/s32[]{:T(128)}, s32[]{:T(128)}) while((s32[]{:T(128)}, f32[4,128,64]{2,1,0:T(8,128)S(1)}, s32[]{:T(128)}, f32[8,4]{1,0:T(8,128)S(1)}, f32[8,4,128,64]{2,3,1,0:T(8,128)}, ...), condition=%wide.region_3.4_spmd.clone, body=%wide.region_2.3_spmd.clone.sunk | while | flops 131076 | bytes 917665 | solution.py:30
  199.2 0.9 constant_dynamic-slice_fusion.3
  200.4 0.9 constant_dynamic-slice_fusion.3
  201.6 0.9 constant_dynamic-slice_fusion.3
  202.8 0.9 constant_dynamic-slice_fusion.3
  207.2 3.9 %fusion.19 = f32[4,256,4,64]{1,3,2,0:T(8,128)} fusion(f32[4,4,256]{2,1,0:T(4,128)S(1)} %copy.123, f32[4,4,256]{2,1,0:T(4,128)S(1)} %fusion.50, f32[4,256,256]{2,1,0:T(8,128)} %fusion.71, pred[256,256]{1,0:T(8,128)(4,1)S(1)} %convert_compare_fusion, f32[4,256,4,64]{1,0,3,2:T(4,128)} %reshape.81, f32[4,256,4,64]{1,3,2,0:T(8,128)S(1)} %bitcast.90, ...), kind=kOutput, calls=%fused_computation.26 | convolution fusion | flops 138936320 | bytes 4308992 | tf_op jit(solution)/shard_map/chts,cshp->cthp/dot_general | solution.py:108
  211.1 2.9 copy.152
  213.9 3.2 reshape.97
  217.2 7.8 %multiply_reduce_fusion = (f32[1024]{0:T(1024)S(1)}, f32[1024,256]{1,0:T(8,128)}) fusion(bf16[4096,256]{1,0:T(8,128)(2,1)} %param.16, bf16[1024,4096]{1,0:T(8,128)(2,1)} %all-gather.7.cloned.1.call-done, f32[4096]{0:T(1024)S(1)} %copy-done.10, f32[1024]{0:T(1024)S(1)} %add_rsqrt_fusion.1, f32[1024,256]{1,0:T(8,128)} %reshape.97, ...), kind=kOutput, calls=%fused_computation.61 | convolution fusion | flops 2167143424 | bytes 13657088 | tf_op jit(solution)/shard_map/dot_general | solution.py:77
  225.0 19.9 %all_to_all.25 = f32[32,1,1024]{2,1,0:T(1,128)S(1)} all-to-all(f32[32,1,1024]{2,1,0:T(1,128)S(1)} %broadcast_in_dim.32), channel_id=1, replica_groups=mesh['seq'=8,'chan'=32] {'chan'}, dimensions={0} | all-to-all | bytes 262144 | tf_op jit(solution)/shard_map/all_to_all | solution.py:35
  245.1 2.2 multiply_convert_fusion
  247.4 4.1 %copy.141 = bf16[256,4096]{0,1:T(8,128)(2,1)} copy(bf16[256,4096]{1,0:T(8,128)(2,1)} %param.25) | data formatting | bytes 4194304 | tf_op args[11]
  251.4 39.8 %all_to_all.26 = bf16[256,32,128]{0,2,1:T(8,128)(2,1)} all-to-all(bf16[256,32,128]{0,2,1:T(8,128)(2,1)} %bitcast.86), channel_id=1, replica_groups=mesh['seq'=8,'chan'=32] {'chan'}, dimensions={1} | all-to-all | bytes 4194304 | tf_op jit(solution)/shard_map/all_to_all | solution.py:133
  291.3 4.1 %copy.142 = bf16[32,256,128]{2,1,0:T(8,128)(2,1)} copy(bf16[32,256,128]{1,2,0:T(8,128)(2,1)} %bitcast.85) | data formatting | bytes 4194304 | tf_op jit(solution)/shard_map/all_to_all | solution.py:133
  295.3 50.5 %all-gather.11.cloned.1.call-done = bf16[1024,8192]{1,0:T(8,128)(2,1)} async-done(((bf16[1024,256]{1,0:T(8,128)(2,1)}), bf16[1024,8192]{1,0:T(8,128)(2,1)}) %all-gather.11.cloned.1.call-update) | async-done | bytes 16777232 | tf_op jit(solution)/shard_map/all_gather | solution.py:135
  345.8 11.6 %fusion.23 = bf16[1024,128]{1,0:T(8,128)(2,1)} fusion(bf16[1024,8192]{1,0:T(8,128)(2,1)} %all-gather.11.cloned.1.call-done, bf16[8192,128]{1,0:T(8,128)(2,1)} %bitcast.89, bf16[1024,128]{1,0:T(8,128)(2,1)S(1)} %copy-done.6), kind=kOutput, calls=%fused_computation.34 | convolution fusion | flops 2147876864 | bytes 19398656 | tf_op jit(solution)/shard_map/dot_general | solution.py:134
  (93 shorter events, 12.2 us)
Async XLA Ops:
  6.5 135.8 %copy-start = (bf16[4096,256]{1,0:T(8,128)(2,1)S(1)}, bf16[4096,256]{1,0:T(8,128)(2,1)}, u32[]{:S(2)}) copy-start(bf16[4096,256]{1,0:T(8,128)(2,1)} %param.17) | copy-start | bytes 6291460
  6.5 71.3 %all-gather.7.cloned.1.call-start = ((), (), s32[]{:S(2)}) async-start(), calls=%async_computation.2 | async-start | bytes 8650752 | tf_op jit(solution)/shard_map/all_gather | solution.py:73
  7.3 122.7 %all-gather.9.cloned.1.call-start = ((), (), s32[]{:S(2)}) async-start(), calls=%async_computation.3 | async-start | bytes 3244032 | tf_op jit(solution)/shard_map/all_gather | solution.py:83
  8.0 189.9 %all-gather.13.cloned.1.call-start = ((), (), s32[]{:S(2)}) async-start(), calls=%async_computation.5 | async-start | bytes 1179648 | tf_op jit(solution)/shard_map/all_gather | solution.py:21
  10.4 119.6 %copy-start.10 = (f32[4096]{0:T(1024)S(1)}, f32[4096]{0:T(1024)}, u32[]{:S(2)}) copy-start(f32[4096]{0:T(1024)} %param.15) | copy-start | bytes 49156
  82.9 58.8 %copy-start.8 = (f32[4]{0:T(128)S(1)}, f32[4]{0:T(128)}, u32[]{:S(2)}) copy-start(f32[4]{0:T(128)} %param.22) | copy-start | bytes 52
  138.1 3.2 copy-start.3
  138.1 20.6 %collective-permute-start.1 = (f32[3,256]{1,0:T(4,128)S(1)}, f32[3,256]{1,0:T(4,128)S(1)}, u32[]{:S(2)}, u32[]{:S(2)}) collective-permute-start(f32[3,256]{1,0:T(4,128)S(1)} %slice.92), channel_id=1, source_target_pairs={{0,32},{32,64},{64,96},{96,128},{128,160},{160,192},{192,224},{1,3... | collective-permute-start | bytes 9224 | tf_op jit(solution)/shard_map/ppermute | solution.py:16
  142.3 9.1 %copy-start.4 = (f32[1024,384]{1,0:T(8,128)S(1)}, f32[1024,384]{1,0:T(8,128)}, u32[]{:S(2)}) copy-start(f32[1024,384]{1,0:T(8,128)} %copy-done.3) | copy-start | bytes 4718596
  148.2 4.3 %collective-permute-start = (bf16[3,256]{1,0:T(4,128)(2,1)S(1)}, bf16[3,256]{1,0:T(4,128)(2,1)S(1)}, u32[]{:S(2)}, u32[]{:S(2)}) collective-permute-start(bf16[3,256]{1,0:T(4,128)(2,1)S(1)} %slice.161), channel_id=1, source_target_pairs={{0,32},{32,64},{64,96},{96,128},{128,160},{160,192},{192,224},{1,3... | collective-permute-start | bytes 4616 | tf_op jit(solution)/shard_map/ppermute | solution.py:16
  153.2 8.7 %copy-start.1 = (f32[1024,256]{1,0:T(8,128)}, f32[1024,256]{1,0:T(8,128)S(1)}, u32[]{:S(2)}) copy-start(f32[1024,256]{1,0:T(8,128)S(1)} %divide_multiply_fusion.1) | copy-start | bytes 3145732
  154.5 9.1 %copy-start.9 = (f32[4]{0:T(128)S(1)}, f32[4]{0:T(128)}, u32[]{:S(2)}) copy-start(f32[4]{0:T(128)} %param.23) | copy-start | bytes 52
  161.9 0.7 copy-start.5
  163.6 182.2 %all-gather.11.cloned.1.call-start = ((), (), s32[]{:S(2)}) async-start(), calls=%async_computation.4 | async-start | bytes 17301504 | tf_op jit(solution)/shard_map/all_gather | solution.py:135
  211.1 6.1 %copy-start.2 = (f32[1024,256]{1,0:T(8,128)S(1)}, f32[1024,256]{1,0:T(8,128)}, u32[]{:S(2)}) copy-start(f32[1024,256]{1,0:T(8,128)} %copy-done.1) | copy-start | bytes 3145732
  217.2 27.9 %copy-start.7 = (f32[256]{0:T(256)S(1)}, f32[256]{0:T(256)}, u32[]{:S(2)}) copy-start(f32[256]{0:T(256)} %param.24) | copy-start | bytes 3076
  251.4 94.4 %copy-start.6 = (bf16[1024,128]{1,0:T(8,128)(2,1)S(1)}, bf16[1024,128]{1,0:T(8,128)(2,1)}, u32[]{:S(2)}) copy-start(bf16[1024,128]{1,0:T(8,128)(2,1)} %param.14) | copy-start | bytes 786436
Sparse Core Ops, SparseCore 0:
  9.8 67.9 all-gather.6
  80.4 49.5 all-gather.8
  163.7 34.1 all-gather.12
  247.5 98.2 all-gather.10
where the time goes:
time: 365 us; the launch traced here: 364 us
  waiting for transfers between devices  186 us (51%)
  blocking collectives  72.1 us (20%)
  matrix products  41.3 us (11%)
  local copies, waits for them, and re-layouts  30.5 us (8%)
  other arithmetic  14.3 us (4%)
  between operations  13.4 us (4%)
  starting transfers between devices  6.52 us (2%)
    all_gather x1, waiting for transfers between devices, local(): gathered = lax.all_gather(tokens, 'chan', axis=1, tiled=True)  67.4 us
    all_gather x1, waiting for transfers between devices, local(): lax.all_gather(shaped, 'chan', axis=1, tiled=True)  50.5 us
    all_gather x1, waiting for transfers between devices, local(): lax.all_gather(state_proj, 'chan', axis=0, tiled=True)  47.1 us
    all_to_all x1, blocking collectives, local(): lax.all_to_all(out_proj, 'chan', split_axis=1, concat_axis=0, tiled=True)  39.8 us
    all_to_all x1, blocking collectives, from_everyone(): lax.all_to_all(jnp.broadcast_to(x[None], (size, *x.shape)), axis, 0, 0, t...  19.9 us
    all_gather x1, waiting for transfers between devices, prefix(): pieces = jax.tree.map(lambda part: lax.all_gather(part, axis), value)  19.2 us
    all_gather x1, blocking collectives, prefix(): pieces = jax.tree.map(lambda part: lax.all_gather(part, axis), value)  12.4 us
    dot_general x1, matrix products, local(): jnp.dot(lax.all_gather(shaped, 'chan', axis=1, tiled=True), column_rows,...  11.6 us
  transfers between devices with their start and end apart: 6, of which 4 were waited for; matrix products, arithmetic and copies ran while one was open for 9% of the time, Pallas kernels for 0%

commit v1 on v0

--- a/solution.py
+++ b/solution.py
@@ -8,6 +8,13 @@
 K = 4
 Q = 256
 DI = 8192
+
+
+def divide_axis_part_in(my_tile):
+    parts_seen = []
+    for _ in range(lax.psum(1, "chan")):
+        parts_seen.append(my_tile)
+    return jnp.concatenate(lax.all_to_all(jnp.stack(parts_seen, axis=0), "chan", 0, 0), axis=1)
 
 
 def from_behind(value, axis, steps):
@@ -70,7 +77,7 @@
     gate_gain,
     out_proj,
 ):
-    gathered = lax.all_gather(tokens, "chan", axis=1, tiled=True)
+    gathered = divide_axis_part_in(tokens)
     widened = gathered.astype(jnp.float32)
     inverse = lax.rsqrt(jnp.mean(widened * widened, axis=1, keepdims=True) + 1e-05)
     normed = (widened * inverse * norm_gain).astype(jnp.bfloat16)

time: 365 us -> 369 us (1.011)
  starting transfers between devices: 6.52 us -> 15.1 us
  waiting for transfers between devices: 186 us -> 180 us
    all_to_all x0 -> x1, waiting for transfers between devices: none -> 105 us  [divide_axis_part_in(): lax.all_to_all(jnp.stack(parts_seen, axis=0), 'chan', 0, 0)]
    all_gather x1 -> x0, waiting for transfers between devices: 67.4 us -> none  [local(): gathered = lax.all_gather(tokens, 'chan', axis=1, tiled=True)]
    all_gather x1, waiting for transfers between devices: 47.1 us -> 0.01 us  [local(): lax.all_gather(state_proj, 'chan', axis=0, tiled=True)]
    all_to_all x0 -> x1, starting transfers between devices: none -> 8.77 us  [divide_axis_part_in(): lax.all_to_all(jnp.stack(parts_seen, axis=0), 'chan', 0, 0)]
    convert_element_type x0 -> x1, other arithmetic: none -> 7.75 us  [local(): normed = (widened * inverse * norm_gain).astype(jnp.bfloat16)]
    another operation x0 -> x1, local copies, waits for them, and re-layouts: none -> 4.32 us  [divide_axis_part_in(): jnp.stack(parts_seen, axis=0)]
  transfers between devices with their start and end apart: 6 -> 6, of which waited for: 4 -> 3; matrix products, arithmetic and copies ran while one was open for 9% -> 6% of each run, Pallas kernels for 0% -> 0%
where the time goes in v1:
time: 369 us; the launch traced here: 368 us
  waiting for transfers between devices  180 us (49%)
  blocking collectives  75.3 us (20%)
  matrix products  37.9 us (10%)
  local copies, waits for them, and re-layouts  28.8 us (8%)
  other arithmetic  17.7 us (5%)
  starting transfers between devices  15.1 us (4%)
  between operations  13.5 us (4%)
    all_to_all x1, waiting for transfers between devices, divide_axis_part_in(): lax.all_to_all(jnp.stack(parts_seen, axis=0), 'chan', 0, 0)  105 us
    all_gather x1, waiting for transfers between devices, local(): lax.all_gather(shaped, 'chan', axis=1, tiled=True)  50.8 us
    all_to_all x1, blocking collectives, local(): lax.all_to_all(out_proj, 'chan', split_axis=1, concat_axis=0, tiled=True)  41 us
    all_gather x1, waiting for transfers between devices, prefix(): pieces = jax.tree.map(lambda part: lax.all_gather(part, axis), value)  22.5 us
    all_to_all x1, blocking collectives, from_everyone(): lax.all_to_all(jnp.broadcast_to(x[None], (size, *x.shape)), axis, 0, 0, t...  20 us
    all_gather x1, blocking collectives, prefix(): pieces = jax.tree.map(lambda part: lax.all_gather(part, axis), value)  14.3 us
    dot_general x1, matrix products, local(): jnp.dot(lax.all_gather(shaped, 'chan', axis=1, tiled=True), column_rows,...  11.8 us
    all_to_all x1, starting transfers between devices, divide_axis_part_in(): lax.all_to_all(jnp.stack(parts_seen, axis=0), 'chan', 0, 0)  8.77 us
  transfers between devices with their start and end apart: 6, of which 3 were waited for; matrix products, arithmetic and copies ran while one was open for 6% of the time, Pallas kernels for 0%

profile of v1, /device:TPU:1, one launch (start us, length us, event | category | flops | bytes accessed | tf_op | source)
XLA Modules:
  0.0 367.9 jit_solution(14272128732492435278)
XLA Ops:
  6.5 1.2 copy.125
  7.8 4.3 %stack.2 = bf16[32,1024,128]{1,2,0:T(8,128)(2,1)} broadcast(bf16[1024,128]{0,1:T(8,128)(2,1)S(1)} %copy.125), dimensions={1,2} | broadcast | bytes 8650752 | tf_op jit(solution)/shard_map/stack | solution.py:17
  12.1 8.8 %all-to-all-start = ((bf16[32,1024,128]{1,2,0:T(8,128)(2,1)}), bf16[32,1024,128]{1,2,0:T(8,128)(2,1)}, u32[]{:S(2)}, u32[]{:S(2)}) async-start(bf16[32,1024,128]{1,2,0:T(8,128)(2,1)} %stack.2), calls=%async_computation | async-start | bytes 16777216 | tf_op jit(solution)/shard_map/all_to_all | solution.py:17
  21.7 105.4 %all-to-all-done = bf16[32,1024,128]{1,2,0:T(8,128)(2,1)} async-done(((bf16[32,1024,128]{1,2,0:T(8,128)(2,1)}), bf16[32,1024,128]{1,2,0:T(8,128)(2,1)}, u32[]{:S(2)}, u32[]{:S(2)}) %all-to-all-start) | async-done | bytes 8388640 | tf_op jit(solution)/shard_map/all_to_all | solution.py:17
  127.2 5.1 %multiply_reduce_fusion = f32[1024]{0:T(1024)S(1)} fusion(bf16[32,1024,128]{1,2,0:T(8,128)(2,1)} %all-to-all-done), kind=kLoop, calls=%fused_computation.7 | loop fusion | flops 12581888 | bytes 8392704 | tf_op jit(solution)/shard_map/reduce_sum | solution.py:82
  132.3 7.7 %fusion.2 = bf16[1024,4096]{0,1:T(8,128)(2,1)} fusion(f32[4096]{0:T(1024)S(1)} %copy-done.7, f32[1024]{0:T(1024)S(1)} %add_rsqrt_fusion.1, bf16[32,1024,128]{1,2,0:T(8,128)(2,1)} %all-to-all-done), kind=kLoop, calls=%fused_computation.6 | loop fusion | flops 16777216 | bytes 16797696 | tf_op jit(solution)/shard_map/convert_element_type | solution.py:83
  140.1 7.9 %fusion.66 = f32[1024,384]{1,0:T(8,128)S(1)} fusion(bf16[1024,4096]{0,1:T(8,128)(2,1)} %fusion.2, bf16[4096,384]{1,0:T(8,128)(2,1)} %all-gather.6.cloned.1.call-done), kind=kOutput, calls=%fused_computation.101 | convolution fusion | flops 3221225472 | bytes 13107200 | tf_op jit(solution)/shard_map/dot_general | solution.py:88
  148.0 1.2 copy-done.2
  150.0 5.8 %fusion.65 = (f32[1024,256]{1,0:T(8,128)S(1)}, bf16[1024,256]{1,0:T(8,128)(2,1)S(1)}) fusion(bf16[1024,4096]{0,1:T(8,128)(2,1)} %fusion.2, bf16[4096,256]{1,0:T(8,128)(2,1)S(1)} %copy-done), kind=kOutput, calls=%fused_computation.100 | convolution fusion | flops 2148007936 | bytes 12058624 | tf_op jit(solution)/shard_map/dot_general | solution.py:85
  155.8 2.9 collective-permute-start
  159.7 3.3 collective-permute-start.1
  163.7 1.3 copy.126
  165.0 1.7 reshape.87
  167.6 0.9 fusion.46
  169.2 14.3 %all-gather.1 = f32[8,1,4]{2,1,0:T(1,128)S(1)} all-gather(f32[1,1,4]{2,1,0:T(1,128)S(1)} %get-tuple-element.179), channel_id=1, replica_groups=mesh['seq'=8,'chan'=32] {'seq'}, dimensions={0}, use_global_device_ids=true | all-gather | bytes 144 | tf_op jit(solution)/shard_map/all_gather | solution.py:28
  183.7 22.5 %all-gather.10.cloned.1.call-done = f32[32,128,64]{1,2,0:T(8,128)} async-done(((f32[4,128,64]{1,2,0:T(8,128)}), f32[32,128,64]{1,2,0:T(8,128)}) %all-gather.10.cloned.1.call-update) | async-done | bytes 1048592 | tf_op jit(solution)/shard_map/all_gather | solution.py:28
  206.3 8.4 %while.14 = (s32[]{:T(128)}, f32[4,128,64]{2,1,0:T(8,128)S(1)}, s32[]{:T(128)}, f32[8,4]{1,0:T(8,128)S(1)}, f32[8,4,128,64]{2,3,1,0:T(8,128)}, /*index=5*/s32[]{:T(128)}, s32[]{:T(128)}) while((s32[]{:T(128)}, f32[4,128,64]{2,1,0:T(8,128)S(1)}, s32[]{:T(128)}, f32[8,4]{1,0:T(8,128)S(1)}, f32[8,4,128,64]{2,3,1,0:T(8,128)}, ...), condition=%wide.region_3.4_spmd.clone, body=%wide.region_2.3_spmd.clone.sunk | while | flops 131076 | bytes 917657 | solution.py:37
  207.5 0.9 constant_dynamic-slice_fusion.3
  208.7 0.9 constant_dynamic-slice_fusion.3
  209.9 0.9 constant_dynamic-slice_fusion.3
  211.1 0.9 constant_dynamic-slice_fusion.3
  215.5 2.4 fusion.18
  217.9 1.9 copy.158
  219.8 2.2 reshape.104
  222.0 8.0 %multiply_reduce_fusion.1 = (f32[1024]{0:T(1024)S(1)}, f32[1024,256]{1,0:T(8,128)}) fusion(bf16[1024,4096]{0,1:T(8,128)(2,1)} %fusion.2, bf16[4096,256]{1,0:T(8,128)(2,1)} %param.16, f32[1024,256]{1,0:T(8,128)} %reshape.104, f32[1024,256]{1,0:T(8,128)S(1)} %copy-done.4, f32[256]{0:T(256)S(1)} %mul.273), kind=kOutput, calls=%fused_computation.60 | convolution fusion | flops 2150366208 | bytes 13636608 | tf_op jit(solution)/shard_map/dot_general | solution.py:84
  230.1 20.0 %all_to_all.30 = f32[32,1,1024]{2,1,0:T(1,128)S(1)} all-to-all(f32[32,1,1024]{2,1,0:T(1,128)S(1)} %broadcast_in_dim.32), channel_id=1, replica_groups=mesh['seq'=8,'chan'=32] {'chan'}, dimensions={0} | all-to-all | bytes 262144 | tf_op jit(solution)/shard_map/all_to_all | solution.py:42
  250.2 2.2 multiply_convert_fusion
  252.4 2.5 copy.147
  254.9 41.0 %all_to_all.31 = bf16[256,32,128]{0,2,1:T(8,128)(2,1)S(1)} all-to-all(bf16[256,32,128]{0,2,1:T(8,128)(2,1)} %bitcast.97), channel_id=1, replica_groups=mesh['seq'=8,'chan'=32] {'chan'}, dimensions={1} | all-to-all | bytes 4194304 | tf_op jit(solution)/shard_map/all_to_all | solution.py:140
  295.9 2.9 copy.148
  298.8 50.8 %all-gather.8.cloned.1.call-done = bf16[1024,8192]{1,0:T(8,128)(2,1)} async-done(((bf16[1024,256]{1,0:T(8,128)(2,1)}), bf16[1024,8192]{1,0:T(8,128)(2,1)}) %all-gather.8.cloned.1.call-update) | async-done | bytes 16777232 | tf_op jit(solution)/shard_map/all_gather | solution.py:142
  349.7 11.8 %fusion.22 = bf16[1024,128]{1,0:T(8,128)(2,1)} fusion(bf16[1024,8192]{1,0:T(8,128)(2,1)} %all-gather.8.cloned.1.call-done, bf16[8192,128]{1,0:T(8,128)(2,1)} %bitcast.100, bf16[1024,128]{1,0:T(8,128)(2,1)S(1)} %copy-done.6), kind=kOutput, calls=%fused_computation.33 | convolution fusion | flops 2147876864 | bytes 19398656 | tf_op jit(solution)/shard_map/dot_general | solution.py:141
  (102 shorter events, 10.4 us)
Async XLA Ops:
  6.5 143.5 %copy-start = (bf16[4096,256]{1,0:T(8,128)(2,1)S(1)}, bf16[4096,256]{1,0:T(8,128)(2,1)}, u32[]{:S(2)}) copy-start(bf16[4096,256]{1,0:T(8,128)(2,1)} %param.17) | copy-start | bytes 6291460
  12.1 9.6 %copy-start.13 = (f32[4]{0:T(128)S(1)}, f32[4]{0:T(128)}, u32[]{:S(2)}) copy-start(f32[4]{0:T(128)} %param.21) | copy-start | bytes 52
  12.1 9.6 %copy-start.8 = (f32[4,256]{1,0:T(4,128)S(1)}, f32[4,256]{1,0:T(4,128)}, u32[]{:S(2)}) copy-start(f32[4,256]{1,0:T(4,128)} %param.19) | copy-start | bytes 12292
  12.1 9.6 %copy-start.9 = (f32[4,256]{1,0:T(4,128)S(1)}, f32[4,256]{1,0:T(4,128)}, u32[]{:S(2)}) copy-start(f32[4,256]{1,0:T(4,128)} %param.20) | copy-start | bytes 12292
  12.1 115.1 %all-to-all-start = ((bf16[32,1024,128]{1,2,0:T(8,128)(2,1)}), bf16[32,1024,128]{1,2,0:T(8,128)(2,1)}, u32[]{:S(2)}, u32[]{:S(2)}) async-start(bf16[32,1024,128]{1,2,0:T(8,128)(2,1)} %stack.2), calls=%async_computation | async-start | bytes 16777216 | tf_op jit(solution)/shard_map/all_to_all | solution.py:17
  20.9 119.2 %all-gather.6.cloned.1.call-start = ((), (), s32[]{:S(2)}) async-start(), calls=%async_computation.3 | async-start | bytes 3244032 | tf_op jit(solution)/shard_map/all_gather | solution.py:90
  21.6 184.7 %all-gather.10.cloned.1.call-start = ((), (), s32[]{:S(2)}) async-start(), calls=%async_computation.5 | async-start | bytes 1179648 | tf_op jit(solution)/shard_map/all_gather | solution.py:28
  21.7 110.6 %copy-start.7 = (f32[4096]{0:T(1024)S(1)}, f32[4096]{0:T(1024)}, u32[]{:S(2)}) copy-start(f32[4096]{0:T(1024)} %param.15) | copy-start | bytes 49156
  140.1 9.5 %copy-start.11 = (f32[4]{0:T(128)S(1)}, f32[4]{0:T(128)}, u32[]{:S(2)}) copy-start(f32[4]{0:T(128)} %param.22) | copy-start | bytes 52
  148.0 1.2 copy-start.2
  155.8 7.2 %collective-permute-start = (bf16[3,256]{1,0:T(4,128)(2,1)S(1)}, bf16[3,256]{1,0:T(4,128)(2,1)S(1)}, u32[]{:S(2)}, u32[]{:S(2)}) collective-permute-start(bf16[3,256]{1,0:T(4,128)(2,1)S(1)} %slice.161), channel_id=1, source_target_pairs={{0,32},{32,64},{64,96},{96,128},{128,160},{160,192},{192,224},{1,3... | collective-permute-start | bytes 4616 | tf_op jit(solution)/shard_map/ppermute | solution.py:23
  158.9 8.0 %slice-start = ((f32[1024,384]{1,0:T(8,128)}), f32[1024,256]{1,0:T(8,128)S(1)}, s32[]{:S(2)}) async-start(f32[1024,384]{1,0:T(8,128)} %copy-done.2), calls=%async_computation.6 | async-start | bytes 2097152 | tf_op jit(solution)/shard_map/slice | solution.py:93
  159.7 7.2 %collective-permute-start.1 = (f32[3,256]{1,0:T(4,128)S(1)}, f32[3,256]{1,0:T(4,128)S(1)}, u32[]{:S(2)}, u32[]{:S(2)}) collective-permute-start(f32[3,256]{1,0:T(4,128)S(1)} %slice.92), channel_id=1, source_target_pairs={{0,32},{32,64},{64,96},{96,128},{128,160},{160,192},{192,224},{1,3... | collective-permute-start | bytes 9224 | tf_op jit(solution)/shard_map/ppermute | solution.py:23
  163.7 3.9 %copy-start.3 = (f32[1024,256]{1,0:T(8,128)}, f32[1024,256]{1,0:T(8,128)S(1)}, u32[]{:S(2)}) copy-start(f32[1024,256]{1,0:T(8,128)S(1)} %divide_multiply_fusion.1) | copy-start | bytes 3145732
  165.0 3.7 copy-start.12
  168.6 181.1 %all-gather.8.cloned.1.call-start = ((), (), s32[]{:S(2)}) async-start(), calls=%async_computation.4 | async-start | bytes 17301504 | tf_op jit(solution)/shard_map/all_gather | solution.py:142
  217.9 4.1 %copy-start.4 = (f32[1024,256]{1,0:T(8,128)S(1)}, f32[1024,256]{1,0:T(8,128)}, u32[]{:S(2)}) copy-start(f32[1024,256]{1,0:T(8,128)} %copy-done.3) | copy-start | bytes 3145732
  222.0 28.1 %copy-start.10 = (f32[256]{0:T(256)S(1)}, f32[256]{0:T(256)}, u32[]{:S(2)}) copy-start(f32[256]{0:T(256)} %param.24) | copy-start | bytes 3076
  222.0 30.4 %copy-start.5 = (bf16[256,4096]{1,0:T(8,128)(2,1)S(1)}, bf16[256,4096]{1,0:T(8,128)(2,1)}, u32[]{:S(2)}) copy-start(bf16[256,4096]{1,0:T(8,128)(2,1)} %param.25) | copy-start | bytes 6291460
  254.9 94.7 %copy-start.6 = (bf16[1024,128]{1,0:T(8,128)(2,1)S(1)}, bf16[1024,128]{1,0:T(8,128)(2,1)}, u32[]{:S(2)}) copy-start(bf16[1024,128]{1,0:T(8,128)(2,1)} %param.14) | copy-start | bytes 786436
  349.7 11.8 %copy-start.1 = (bf16[4096,256]{1,0:T(8,128)(2,1)S(1)}, bf16[4096,256]{1,0:T(8,128)(2,1)}, u32[]{:S(2)}) copy-start(bf16[4096,256]{1,0:T(8,128)(2,1)} %param.17) | copy-start | bytes 6291460
Sparse Core Ops, SparseCore 0:
  24.2 105.6 all-gather.5
  168.7 37.5 all-gather.9
  252.6 97.0 all-gather.7
